TPU v7x, 32 devices: a whole 2x2x4 slice. The times are simulated.
32 devices in a mesh: seq: 16 (over z, y, x), head: 2 (over core).
Axes of the slice: x: 2, y: 2, z: 4, core: 2. Of those that a mesh axis runs over, the one named last changes fastest.
Arguments:
- queries: bfloat16 [4096, 64, 192], P('seq', 'head'), may hold values from -50 to 50
- grad_out: bfloat16 [4096, 64, 128], P('seq', 'head'), may hold values from -6 to 6
- latent: bfloat16 [4096, 576], P('seq'), may hold values from -18 to 18
- w_uk: bfloat16 [64, 512, 128], P('head'), may hold values from -0.25 to 0.25
- w_uv: bfloat16 [64, 512, 128], P('head'), may hold values from -0.25 to 0.25
- doc_start: int32 [4096], P('seq'), may hold values from 0 to 4095, as said below
Outputs:
- grad_query: bfloat16 [4096, 64, 192], P('seq', 'head')
- grad_latent: float32 [4096, 576], P(('seq', 'head'))
Inputs may be any that keep to these rules, and one draw needn't show every extreme that they name: doc_start[t] is the first position of the document that holds position t; documents follow one another, each of 1 to 768 positions, and one is exactly 768 long.
All inputs are finite; a program needn't handle non-finite values.
Results may differ from a plain program's by a relative error of at most 0.008.
Values may be sent and summed in bfloat16 or wider, within the bound.
A program may use at most 192 MiB of HBM per device.

v0:
```python
import jax
import jax.numpy as jnp
from jax import lax
from jax.sharding import PartitionSpec as P

BACK = 3


def from_behind(block, axis, distance):
    devices = range(lax.axis_size(axis))
    route = [(i - distance, i) for i in devices if i - distance in devices]
    return lax.ppermute(block, axis, route)


def send_back(stacked):
    total = stacked[BACK]
    for reach in range(1, BACK + 1):
        total = total + from_behind(
            stacked[BACK - reach].astype(jnp.bfloat16), "seq", -reach
        ).astype(jnp.float32)
    return total


def shards(queries, grad_out, latent, w_uk, w_uv, doc_start):
    tokens = latent.shape[0]
    width = latent.shape[1]
    latw = w_uk.shape[1]
    nope = w_uk.shape[2]
    rope = width - latw
    factor = queries.shape[2] ** (-0.5)
    packed = latent.reshape(tokens // 2, 2 * width)
    received = [from_behind(packed, "seq", level + 1) for level in range(BACK)]
    keys = jnp.concatenate([piece.reshape(tokens, width) for piece in received[::-1]] + [latent], 0)
    span = keys.shape[0]
    index = lax.axis_index("seq")
    qpos = index * tokens + jnp.arange(tokens, dtype=jnp.int32)
    kpos = (index - BACK) * tokens + jnp.arange(span, dtype=jnp.int32)
    visible = (kpos[None, :] >= doc_start[:, None]) & (kpos[None, :] <= qpos[:, None])
    q_abs = jnp.einsum(
        "thn,hln->thl", queries[:, :, :nope], w_uk, preferred_element_type=jnp.float32
    ).astype(jnp.bfloat16)
    qcat = jnp.concatenate([q_abs, queries[:, :, nope:]], -1)
    scores = jnp.einsum("thc,uc->htu", qcat, keys, preferred_element_type=jnp.float32) * factor
    scores = jnp.where(visible[None], scores, -jnp.inf)
    top = jnp.max(scores, -1, keepdims=True)
    expo = jnp.exp(scores - top)
    probs = (expo / jnp.sum(expo, -1, keepdims=True)).astype(jnp.bfloat16)
    grad_lat = jnp.einsum(
        "thv,hlv->thl", grad_out, w_uv, preferred_element_type=jnp.float32
    ).astype(jnp.bfloat16)
    values = keys[:, :latw]
    o_lat = jnp.einsum("htu,ul->thl", probs, values, preferred_element_type=jnp.float32)
    delta = jnp.sum(grad_lat.astype(jnp.float32) * o_lat, -1)
    dprob = jnp.einsum("thl,ul->htu", grad_lat, values, preferred_element_type=jnp.float32)
    dscore = (probs.astype(jnp.float32) * (dprob - delta.T[:, :, None])).astype(jnp.bfloat16)
    dq_cat = jnp.einsum("htu,uc->thc", dscore, keys, preferred_element_type=jnp.float32) * factor
    dq_abs = dq_cat[:, :, :latw].astype(jnp.bfloat16)
    dq_nope = jnp.einsum("thl,hln->thn", dq_abs, w_uk, preferred_element_type=jnp.float32)
    grad_query = jnp.concatenate([dq_nope, dq_cat[:, :, latw:]], -1).astype(jnp.bfloat16)
    dkey = jnp.einsum("htu,thc->uc", dscore, qcat, preferred_element_type=jnp.float32) * factor
    dvalue = jnp.einsum("htu,thl->ul", probs, grad_lat, preferred_element_type=jnp.float32)
    dkey = dkey + jnp.pad(dvalue, ((0, 0), (0, rope)))
    stacked = dkey.reshape(BACK + 1, tokens // 2, 2 * width)
    returned = send_back(stacked)
    result = lax.psum_scatter(returned, "head", scatter_dimension=0, tiled=True)
    grad_latent = result.reshape(-1, width)
    return (grad_query, grad_latent)


def solution(mesh):
    placed = (
        P("seq", "head", None),
        P("seq", "head", None),
        P("seq", None),
        P("head", None, None),
        P("head", None, None),
        P("seq"),
    )
    return jax.shard_map(
        shards,
        mesh=mesh,
        in_specs=placed,
        out_specs=(P("seq", "head", None), P(("seq", "head"), None)),
        check_vma=False,
    )
```

profile of v0, /device:TPU:12, one launch (start us, length us, event | category | flops | bytes accessed | tf_op | source)
XLA Modules:
  0.0 242.4 jit_solution(4398525858641746912)
XLA Ops:
  7.2 1.3 copy.18
  8.8 4.4 %collective-permute-start = (bf16[128,1152]{1,0:T(8,128)(2,1)S(1)}, bf16[128,1152]{1,0:T(8,128)(2,1)}, u32[]{:S(2)}, u32[]{:S(2)}) collective-permute-start(bf16[128,1152]{1,0:T(8,128)(2,1)S(1)} %reshape.96), channel_id=1, source_target_pairs={{0,6},{2,8},{4,10},{6,12},{8,14},{10,16},{12,18},{14,20},{16,22},{... | collective-permute-start | bytes 884744 | tf_op jit(solution)/shard_map/ppermute | solution.py:12
  13.2 3.4 %collective-permute-start.1 = (bf16[128,1152]{1,0:T(8,128)(2,1)S(1)}, bf16[128,1152]{1,0:T(8,128)(2,1)}, u32[]{:S(2)}, u32[]{:S(2)}) collective-permute-start(bf16[128,1152]{1,0:T(8,128)(2,1)S(1)} %reshape.96), channel_id=1, source_target_pairs={{0,4},{2,6},{4,8},{6,10},{8,12},{10,14},{12,16},{14,18},{16,20},{1... | collective-permute-start | bytes 884744 | tf_op jit(solution)/shard_map/ppermute | solution.py:12
  16.6 2.5 %collective-permute-start.2 = (bf16[128,1152]{1,0:T(8,128)(2,1)S(1)}, bf16[128,1152]{1,0:T(8,128)(2,1)S(1)}, u32[]{:S(2)}, u32[]{:S(2)}) collective-permute-start(bf16[128,1152]{1,0:T(8,128)(2,1)S(1)} %reshape.96), channel_id=1, source_target_pairs={{0,2},{2,4},{4,6},{6,8},{8,10},{10,12},{12,14},{14,16},{16,18},{18... | collective-permute-start | bytes 884744 | tf_op jit(solution)/shard_map/ppermute | solution.py:12
  19.1 2.3 slice.37
  21.4 8.4 %convert_bitcast_fusion = bf16[256,32,512]{0,2,1:T(8,128)(2,1)} fusion(bf16[32,512,128]{2,1,0:T(8,128)(2,1)} %param.9, bf16[256,32,192]{0,2,1:T(8,128)(2,1)} %param.6), kind=kOutput, calls=%fused_computation.20 | convolution fusion | flops 1077936128 | bytes 14680064 | tf_op jit(solution)/shard_map/thn,hln->thl/dot_general | solution.py:39
  29.9 8.0 %convolution_convert_fusion = bf16[32,512,256]{2,1,0:T(8,128)(2,1)} fusion(bf16[32,512,128]{2,1,0:T(8,128)(2,1)} %param.10, bf16[256,32,128]{2,1,0:T(8,128)(2,1)S(1)} %copy-done), kind=kOutput, calls=%fused_computation.21 | convolution fusion | flops 1077936128 | bytes 14680064 | tf_op jit(solution)/shard_map/thv,hlv->thl/dot_general | solution.py:48
  41.4 22.5 %fusion.14 = f32[1024,256,32]{1,0,2:T(8,128)} fusion(bf16[256,32,64]{0,2,1:T(8,128)(2,1)} %slice.37, bf16[256,32,512]{0,2,1:T(8,128)(2,1)} %convert_bitcast_fusion, bf16[256,576]{0,1:T(8,128)(2,1)S(1)} %copy-done.4, bf16[256,576]{0,1:T(8,128)(2,1)S(1)} %copy.21, bf16[256,576]{0,1:T(8,128)(2,1)S(1)} %copy.20, bf16[256,576]{0,1:T(8,128)(2,1)S(1)} %copy.19), kind=kOutput, calls=%fused_computation.23 | convolution fusion | flops 9687269376 | bytes 44171264 | tf_op jit(solution)/shard_map/thc,uc->htu/dot_general | solution.py:43
  63.9 33.2 %fusion.31 = (f32[32,256]{1,0:T(8,128)S(1)}, f32[32,256,1024]{1,2,0:T(8,128)}) fusion(f32[1024,256,32]{1,0,2:T(8,128)} %fusion.14, pred[256,1024]{0,1:T(8,128)(4,1)S(1)} %compare_and_fusion), kind=kOutput, calls=%fused_computation.45 | output fusion | flops 50332672 | bytes 67403776 | tf_op jit(solution)/shard_map/sub | solution.py:46
  97.1 12.2 %divide_convert_fusion = bf16[32,256,1024]{1,2,0:T(8,128)(2,1)S(1)} fusion(f32[32,256,1024]{1,2,0:T(8,128)} %get-tuple-element.8, f32[32,256]{1,0:T(8,128)S(1)} %get-tuple-element.7), kind=kLoop, calls=%fused_computation.5 | loop fusion | flops 16777216 | bytes 50364416 | tf_op jit(solution)/shard_map/convert_element_type | solution.py:47
  109.3 15.4 %fusion.21 = f32[1024,512]{0,1:T(8,128)} fusion(bf16[32,256,1024]{1,2,0:T(8,128)(2,1)S(1)} %divide_convert_fusion, bf16[32,512,256]{2,1,0:T(8,128)(2,1)} %convolution_convert_fusion), kind=kOutput, calls=%fused_computation.31 | convolution fusion | flops 8589934592 | bytes 27262976 | tf_op jit(solution)/shard_map/htu,thl->ul/dot_general | solution.py:61
  124.8 11.8 %fusion.4 = f32[256,32]{0,1:T(8,128)S(1)} fusion(bf16[32,256,1024]{1,2,0:T(8,128)(2,1)S(1)} %divide_convert_fusion, bf16[32,512,256]{2,1,0:T(8,128)(2,1)} %convolution_convert_fusion, bf16[1024,576]{0,1:T(8,128)(2,1)S(1)} %pad_maximum_fusion.6), kind=kOutput, calls=%fused_computation.10 | convolution fusion | flops 8602509312 | bytes 26247168 | tf_op jit(solution)/shard_map/htu,ul->thl/dot_general | solution.py:52
  136.6 18.9 %fusion.2 = bf16[32,256,1024]{1,2,0:T(8,128)(2,1)} fusion(bf16[32,256,1024]{1,2,0:T(8,128)(2,1)} %copy-done.2, f32[32,256]{1,0:T(8,128)S(1)} %bitcast.59, bf16[32,512,256]{2,1,0:T(8,128)(2,1)} %convolution_convert_fusion, bf16[1024,576]{0,1:T(8,128)(2,1)S(1)} %pad_maximum_fusion.6), kind=kOutput, calls=%fused_computation.3 | convolution fusion | flops 8623489024 | bytes 43024384 | tf_op jit(solution)/shard_map/thl,ul->htu/dot_general | solution.py:54
  155.4 18.9 %fusion.32 = (bf16[1024,576]{0,1:T(8,128)(2,1)}, f32[1024,576]{0,1:T(8,128)}) fusion(f32[1024,512]{0,1:T(8,128)} %fusion.21, bf16[32,256,1024]{1,2,0:T(8,128)(2,1)} %fusion.2, bf16[256,32,64]{0,2,1:T(8,128)(2,1)} %slice.37, bf16[256,32,512]{0,2,1:T(8,128)(2,1)} %convert_bitcast_fusion), kind=kOutput, calls=%fused_computation.46 | convolution fusion | flops 9684320256 | bytes 31850496 | tf_op jit(solution)/shard_map/htu,thc->uc/dot_general | solution.py:60
  176.8 4.5 %collective-permute-start.3 = (bf16[128,1152]{1,0:T(8,128)(2,1)}, bf16[128,1152]{1,0:T(8,128)(2,1)}, u32[]{:S(2)}, u32[]{:S(2)}) collective-permute-start(bf16[128,1152]{1,0:T(8,128)(2,1)} %convert_element_type.57), channel_id=1, source_target_pairs={{2,0},{4,2},{6,4},{8,6},{10,8},{12,10},{14,12},{16,14},{18,16},{20... | collective-permute-start | bytes 884744 | tf_op jit(solution)/shard_map/ppermute | solution.py:12
  181.8 3.3 %collective-permute-start.4 = (bf16[128,1152]{1,0:T(8,128)(2,1)S(1)}, bf16[128,1152]{1,0:T(8,128)(2,1)}, u32[]{:S(2)}, u32[]{:S(2)}) collective-permute-start(bf16[128,1152]{1,0:T(8,128)(2,1)S(1)} %convert_element_type.59), channel_id=1, source_target_pairs={{4,0},{6,2},{8,4},{10,6},{12,8},{14,10},{16,12},{18,14},{20,16},{2... | collective-permute-start | bytes 884744 | tf_op jit(solution)/shard_map/ppermute | solution.py:12
  185.5 1.9 collective-permute-start.5
  189.0 10.0 %collective-permute-done.4 = bf16[128,1152]{1,0:T(8,128)(2,1)} collective-permute-done((bf16[128,1152]{1,0:T(8,128)(2,1)S(1)}, bf16[128,1152]{1,0:T(8,128)(2,1)}, u32[]{:S(2)}, u32[]{:S(2)}) %collective-permute-start.4) | collective-permute-done | bytes 294944 | tf_op jit(solution)/shard_map/ppermute | solution.py:12
  199.0 4.2 %collective-permute-done.5 = bf16[128,1152]{1,0:T(8,128)(2,1)} collective-permute-done((bf16[128,1152]{1,0:T(8,128)(2,1)S(1)}, bf16[128,1152]{1,0:T(8,128)(2,1)}, u32[]{:S(2)}, u32[]{:S(2)}) %collective-permute-start.5) | collective-permute-done | bytes 294944 | tf_op jit(solution)/shard_map/ppermute | solution.py:12
  203.2 2.1 convert_add_fusion
  205.3 13.5 %fusion.15 = bf16[256,32,576]{0,2,1:T(8,128)(2,1)S(1)} fusion(bf16[32,256,1024]{1,2,0:T(8,128)(2,1)} %fusion.2, bf16[256,576]{0,1:T(8,128)(2,1)S(1)} %copy-done.4, bf16[256,576]{0,1:T(8,128)(2,1)S(1)} %copy-done.6, bf16[256,576]{0,1:T(8,128)(2,1)S(1)} %copy.20, bf16[256,576]{0,1:T(8,128)(2,1)S(1)} %copy.19), kind=kOutput, calls=%fused_computation.24 | convolution fusion | flops 9677832192 | bytes 27394048 | tf_op jit(solution)/shard_map/htu,uc->thc/dot_general | solution.py:56
  218.9 3.6 %copy-done.3 = bf16[256,32,576]{0,2,1:T(8,128)(2,1)} copy-done((bf16[256,32,576]{0,2,1:T(8,128)(2,1)}, bf16[256,32,576]{0,2,1:T(8,128)(2,1)S(1)}, u32[]{:S(2)}) %copy-start.3) | copy-done | bytes 9437208
  222.5 7.6 %convert_bitcast_fusion.1 = bf16[256,32,128]{0,2,1:T(8,128)(2,1)} fusion(bf16[32,512,128]{2,1,0:T(8,128)(2,1)} %param.9, bf16[256,32,576]{0,2,1:T(8,128)(2,1)} %copy-done.3), kind=kOutput, calls=%fused_computation.29 | convolution fusion | flops 1074790400 | bytes 14680064 | tf_op jit(solution)/shard_map/thl,hln->thn/dot_general | solution.py:58
  230.1 3.5 %pad_maximum_fusion.3 = bf16[256,32,192]{0,2,1:T(8,128)(2,1)} fusion(bf16[256,32,64]{0,2,1:T(8,128)(2,1)S(1)} %slice-done, bf16[256,32,128]{0,2,1:T(8,128)(2,1)} %convert_bitcast_fusion.1), kind=kLoop, calls=%fused_computation.25 | loop fusion | flops 6291456 | bytes 6291456 | tf_op jit(solution)/shard_map/concatenate | solution.py:59
  (47 shorter events, 10.6 us)
Async XLA Ops:
  7.2 22.7 %copy-start = (bf16[256,32,128]{2,1,0:T(8,128)(2,1)S(1)}, bf16[256,32,128]{2,1,0:T(8,128)(2,1)}, u32[]{:S(2)}) copy-start(bf16[256,32,128]{2,1,0:T(8,128)(2,1)} %param.7) | copy-start | bytes 6291460
  7.2 226.4 %reduce-scatter.2.cloned.1.call-start = ((), (), s32[]{:S(2)}) async-start(), calls=%async_computation.1 | async-start | bytes 884736 | tf_op jit(solution)/shard_map/reduce_scatter | solution.py:65
  8.8 29.3 %collective-permute-start = (bf16[128,1152]{1,0:T(8,128)(2,1)S(1)}, bf16[128,1152]{1,0:T(8,128)(2,1)}, u32[]{:S(2)}, u32[]{:S(2)}) collective-permute-start(bf16[128,1152]{1,0:T(8,128)(2,1)S(1)} %reshape.96), channel_id=1, source_target_pairs={{0,6},{2,8},{4,10},{6,12},{8,14},{10,16},{12,18},{14,20},{16,22},{... | collective-permute-start | bytes 884744 | tf_op jit(solution)/shard_map/ppermute | solution.py:12
  13.2 26.3 %collective-permute-start.1 = (bf16[128,1152]{1,0:T(8,128)(2,1)S(1)}, bf16[128,1152]{1,0:T(8,128)(2,1)}, u32[]{:S(2)}, u32[]{:S(2)}) collective-permute-start(bf16[128,1152]{1,0:T(8,128)(2,1)S(1)} %reshape.96), channel_id=1, source_target_pairs={{0,4},{2,6},{4,8},{6,10},{8,12},{10,14},{12,16},{14,18},{16,20},{1... | collective-permute-start | bytes 884744 | tf_op jit(solution)/shard_map/ppermute | solution.py:12
  16.6 24.2 %collective-permute-start.2 = (bf16[128,1152]{1,0:T(8,128)(2,1)S(1)}, bf16[128,1152]{1,0:T(8,128)(2,1)S(1)}, u32[]{:S(2)}, u32[]{:S(2)}) collective-permute-start(bf16[128,1152]{1,0:T(8,128)(2,1)S(1)} %reshape.96), channel_id=1, source_target_pairs={{0,2},{2,4},{4,6},{6,8},{8,10},{10,12},{12,14},{14,16},{16,18},{18... | collective-permute-start | bytes 884744 | tf_op jit(solution)/shard_map/ppermute | solution.py:12
  29.8 8.0 %copy-start.7 = (s32[256]{0:T(256)S(1)}, s32[256]{0:T(256)}, u32[]{:S(2)}) copy-start(s32[256]{0:T(256)} %param.11) | copy-start | bytes 3076
  29.8 11.4 %copy-start.4 = (bf16[256,576]{0,1:T(8,128)(2,1)S(1)}, bf16[256,576]{0,1:T(8,128)(2,1)}, u32[]{:S(2)}) copy-start(bf16[256,576]{0,1:T(8,128)(2,1)} %param.8) | copy-start | bytes 884740
  41.2 22.6 %copy-start.5 = (bf16[256,576]{0,1:T(8,128)(2,1)}, bf16[256,576]{0,1:T(8,128)(2,1)S(1)}, u32[]{:S(2)}) copy-start(bf16[256,576]{0,1:T(8,128)(2,1)S(1)} %copy.21) | copy-start | bytes 884740
  109.3 15.5 %copy-start.2 = (bf16[32,256,1024]{1,2,0:T(8,128)(2,1)}, bf16[32,256,1024]{1,2,0:T(8,128)(2,1)S(1)}, u32[]{:S(2)}) copy-start(bf16[32,256,1024]{1,2,0:T(8,128)(2,1)S(1)} %divide_convert_fusion) | copy-start | bytes 50331652
  174.4 30.9 %copy-start.6 = (bf16[256,576]{0,1:T(8,128)(2,1)S(1)}, bf16[256,576]{0,1:T(8,128)(2,1)}, u32[]{:S(2)}) copy-start(bf16[256,576]{0,1:T(8,128)(2,1)} %copy-done.5) | copy-start | bytes 884740
  176.8 12.2 %collective-permute-start.3 = (bf16[128,1152]{1,0:T(8,128)(2,1)}, bf16[128,1152]{1,0:T(8,128)(2,1)}, u32[]{:S(2)}, u32[]{:S(2)}) collective-permute-start(bf16[128,1152]{1,0:T(8,128)(2,1)} %convert_element_type.57), channel_id=1, source_target_pairs={{2,0},{4,2},{6,4},{8,6},{10,8},{12,10},{14,12},{16,14},{18,16},{20... | collective-permute-start | bytes 884744 | tf_op jit(solution)/shard_map/ppermute | solution.py:12
  181.8 17.3 %collective-permute-start.4 = (bf16[128,1152]{1,0:T(8,128)(2,1)S(1)}, bf16[128,1152]{1,0:T(8,128)(2,1)}, u32[]{:S(2)}, u32[]{:S(2)}) collective-permute-start(bf16[128,1152]{1,0:T(8,128)(2,1)S(1)} %convert_element_type.59), channel_id=1, source_target_pairs={{4,0},{6,2},{8,4},{10,6},{12,8},{14,10},{16,12},{18,14},{20,16},{2... | collective-permute-start | bytes 884744 | tf_op jit(solution)/shard_map/ppermute | solution.py:12
  185.5 17.6 %collective-permute-start.5 = (bf16[128,1152]{1,0:T(8,128)(2,1)S(1)}, bf16[128,1152]{1,0:T(8,128)(2,1)}, u32[]{:S(2)}, u32[]{:S(2)}) collective-permute-start(bf16[128,1152]{1,0:T(8,128)(2,1)S(1)} %convert_element_type.61), channel_id=1, source_target_pairs={{6,0},{8,2},{10,4},{12,6},{14,8},{16,10},{18,12},{20,14},{22,16},{... | collective-permute-start | bytes 884744 | tf_op jit(solution)/shard_map/ppermute | solution.py:12
  218.9 3.6 %copy-start.3 = (bf16[256,32,576]{0,2,1:T(8,128)(2,1)}, bf16[256,32,576]{0,2,1:T(8,128)(2,1)S(1)}, u32[]{:S(2)}) copy-start(bf16[256,32,576]{0,2,1:T(8,128)(2,1)S(1)} %fusion.15) | copy-start | bytes 28311556
  222.5 13.1 %copy-start.1 = (bf16[256,32,128]{2,1,0:T(8,128)(2,1)S(1)}, bf16[256,32,128]{2,1,0:T(8,128)(2,1)}, u32[]{:S(2)}) copy-start(bf16[256,32,128]{2,1,0:T(8,128)(2,1)} %param.7) | copy-start | bytes 6291460
  222.5 7.6 %slice-start = ((bf16[256,32,576]{0,2,1:T(8,128)(2,1)}), bf16[256,32,64]{0,2,1:T(8,128)(2,1)S(1)}, s32[]{:S(2)}) async-start(bf16[256,32,576]{0,2,1:T(8,128)(2,1)} %copy-done.3), calls=%async_computation.2 | async-start | bytes 2097152 | tf_op jit(solution)/shard_map/slice | solution.py:59
Sparse Core Ops, SparseCore 0:
  205.4 6.3 reduce-scatter.1
where the time goes:
time: 243 us; the launch traced here: 242 us
  matrix products  125 us (51%)
  other arithmetic  51.5 us (21%)
  starting transfers between devices  20.1 us (8%)
  local copies, waits for them, and re-layouts  17.4 us (7%)
  between operations  14.3 us (6%)
  waiting for transfers between devices  14.2 us (6%)
    sub x1, other arithmetic, shards(): expo = jnp.exp(scores - top)  33.2 us
    dot_general x1, matrix products, shards(): jnp.einsum('thc,uc->htu', qcat, keys, preferred_element_type=jnp.float32)  22.5 us
    ppermute x6, starting transfers between devices, from_behind(): return lax.ppermute(block, axis, route)  20 us
    dot_general x1, matrix products, shards(): jnp.einsum('htu,thc->uc', dscore, qcat, preferred_element_type=jnp.float32)  18.9 us
    dot_general x1, matrix products, shards(): jnp.einsum('thl,ul->htu', grad_lat, values, preferred_element_type=jnp.fl...  18.9 us
    dot_general x1, matrix products, shards(): jnp.einsum('htu,thl->ul', probs, grad_lat, preferred_element_type=jnp.flo...  15.4 us
    ppermute x6, waiting for transfers between devices, from_behind(): return lax.ppermute(block, axis, route)  14.2 us
    dot_general x1, matrix products, shards(): jnp.einsum('htu,uc->thc', dscore, keys, preferred_element_type=jnp.float32)  13.5 us
  transfers between devices with their start and end apart: 7, of which 2 were waited for; matrix products, arithmetic and copies ran while one was open for 20% of the time, Pallas kernels for 0%

commit v1 on v0

v1 whole, which is shorter than its diff:
```python
import functools
import math

import jax
import jax.numpy as jnp
from jax import lax
from jax.experimental import pallas as pl
from jax.experimental.pallas import tpu as pltpu
from jax.sharding import PartitionSpec as P

BACK = 3
LANES = 128
PAIR = 2
HIDDEN = -1e30
F32 = jnp.float32
BF16 = jnp.bfloat16
NN = (((1,), (0,)), ((), ()))
NT = (((1,), (1,)), ((), ()))


def dot(a, b, dims=NN):
    return lax.dot_general(a, b, dims, preferred_element_type=F32)


def kernel(tokens, nope, latw, factor, halves, counts, side, starts, q_ref, g_ref, uk_ref, uv_ref, kt_ref,
           gq_ref, *refs):
    *sums, k_ref, bias_ref, acc_ref, qc_ref, gl_ref, dqa_ref = refs
    step = pl.program_id(0)
    width, span = kt_ref.shape
    blocks = tokens // LANES

    @pl.when(step == 0)
    def _():
        acc_ref[...] = jnp.zeros_like(acc_ref)
        for j in range(span // LANES):
            part = pl.ds(j * LANES, LANES)
            k_ref[part, :] = kt_ref[:, part].T
            kpos = lax.broadcasted_iota(jnp.int32, (LANES, tokens), 0) + j * LANES
            qpos = lax.broadcasted_iota(jnp.int32, (LANES, tokens), 1) + (span - tokens)
            seen = (kpos >= starts[...]) & (kpos <= qpos)
            bias_ref[part, :] = jnp.where(seen, 0.0, HIDDEN)

    for i in range(PAIR):
        columns = pl.ds(i * LANES, LANES)
        q_abs = dot(uk_ref[i], q_ref[i, :nope, :]).astype(BF16)
        grad_lat = dot(uv_ref[i], g_ref[i], NT).astype(BF16)
        for b in range(blocks):
            here = slice(b * LANES, (b + 1) * LANES)
            qc_ref[b, :latw, columns] = q_abs[:, here]
            qc_ref[b, latw:, columns] = q_ref[i, nope:, here]
            gl_ref[b, :, columns] = grad_lat[:, here]

    def attend(b, count):
        end = span - (blocks - 1 - b) * LANES
        rows = slice(end - count * LANES, end)
        here = slice(b * LANES, (b + 1) * LANES)
        bias = bias_ref[rows, here]
        scores = dot(k_ref[rows, :], qc_ref[b]) + jnp.concatenate([bias] * PAIR, 1)
        dprob = dot(k_ref[rows, :latw], gl_ref[b])
        top = jnp.max(scores, 0, keepdims=True)
        expo = jnp.exp2((scores - top) * (factor * math.log2(math.e)))
        probs = (expo * (1.0 / jnp.sum(expo, 0, keepdims=True))).astype(BF16)
        wide = probs.astype(F32)
        delta = jnp.sum(wide * dprob, 0, keepdims=True)
        dscore = (wide * (dprob - delta)).astype(BF16)
        dvalue = dot(gl_ref[b], probs, NT) * (1.0 / factor)
        dq = dot(kt_ref[:, rows], dscore) * factor
        dkey = dot(qc_ref[b], dscore, NT)
        acc_ref[:latw, rows] += dkey[:latw] + dvalue
        acc_ref[latw:, rows] += dkey[latw:]
        for i in range(PAIR):
            columns = slice(i * LANES, (i + 1) * LANES)
            dqa_ref[i, :, here] = dq[:latw, columns].astype(BF16)
            gq_ref[i, nope:, here] = dq[latw:, columns].astype(BF16)

    most = span // LANES - blocks + 1
    sizes = sorted({2, 4, *range(5, most), most})
    for b in range(blocks):
        least = 0
        for size in sizes:
            count = counts[b]
            fits = (count > least) & (count <= size)
            pl.when(fits)(functools.partial(attend, b, size))
            least = size

    for i in range(PAIR):
        gq_ref[i, :nope, :] = dot(uk_ref[i].T, dqa_ref[i]).astype(BF16)

    @pl.when(step == pl.num_programs(0) - 1)
    def _():
        if not halves:
            for r in range(span // tokens):
                sums[0][r] = acc_ref[:, r * tokens:(r + 1) * tokens] * factor
            return
        mine_ref, theirs_ref = sums
        half = tokens // 2
        for r in range(span // tokens):
            own = pl.ds(pl.multiple_of(r * tokens + side[0] * half, half), half)
            other = pl.ds(pl.multiple_of(r * tokens + (1 - side[0]) * half, half), half)
            mine_ref[r] = acc_ref[:, own] * factor
            theirs_ref[r] = (acc_ref[:, other] * factor).astype(BF16)


def shift(block, axis, distance):
    devices = range(lax.axis_size(axis))
    route = [(i - distance, i) for i in devices if i - distance in devices]
    return lax.ppermute(block, axis, route)


def shards(queries, grad_out, latent, w_uk, w_uv, doc_start):
    tokens, heads, depth = queries.shape
    width = latent.shape[1]
    latw, nope = w_uk.shape[1:]
    vdim = w_uv.shape[2]
    span = (BACK + 1) * tokens
    blocks = tokens // LANES
    factor = depth ** (-0.5)
    own = latent.T
    received = [shift(own, "seq", level) for level in range(BACK, 0, -1)]
    keys = jnp.concatenate(received + [own], 1)
    starts = doc_start - (lax.axis_index("seq") - BACK) * tokens
    ends = (span - tokens) // LANES + 1 + jnp.arange(blocks, dtype=jnp.int32)
    counts = ends - starts[::LANES] // LANES
    side = lax.axis_index("head").astype(jnp.int32)[None]
    halves = lax.axis_size("head") == 2
    share = tokens // 2 if halves else tokens
    sums = [F32, BF16] if halves else [F32]

    def per_pair(*shape):
        return pl.BlockSpec((PAIR,) + shape, lambda p, *_: (p, 0, 0))

    def whole(*shape):
        return pl.BlockSpec(shape, lambda p, *_: (0,) * len(shape))

    grad_q, mine, *theirs = pl.pallas_call(
        functools.partial(kernel, tokens, nope, latw, factor, halves),
        grid_spec=pltpu.PrefetchScalarGridSpec(
            num_scalar_prefetch=2,
            grid=(heads // PAIR,),
            in_specs=[
                whole(1, tokens),
                per_pair(depth, tokens),
                per_pair(tokens, vdim),
                per_pair(latw, nope),
                per_pair(latw, vdim),
                whole(width, span),
            ],
            out_specs=[
                per_pair(depth, tokens),
                *[whole(BACK + 1, width, share) for _ in sums],
            ],
            scratch_shapes=[
                pltpu.VMEM((span, width), BF16),
                pltpu.VMEM((span, tokens), F32),
                pltpu.VMEM((width, span), F32),
                pltpu.VMEM((blocks, width, PAIR * LANES), BF16),
                pltpu.VMEM((blocks, latw, PAIR * LANES), BF16),
                pltpu.VMEM((PAIR, latw, tokens), BF16),
            ],
        ),
        out_shape=[
            jax.ShapeDtypeStruct((heads, depth, tokens), BF16),
            *[jax.ShapeDtypeStruct((BACK + 1, width, share), kind) for kind in sums],
        ],
        compiler_params=pltpu.CompilerParams(
            dimension_semantics=("arbitrary",), vmem_limit_bytes=60 * 1024 * 1024
        ),
        name="attend",
    )(
        counts,
        side,
        starts[None, :],
        queries.transpose(1, 2, 0),
        grad_out.transpose(1, 0, 2),
        w_uk,
        w_uv,
        keys,
    )
    grad_query = grad_q.transpose(2, 0, 1)
    summed = mine
    if halves:
        summed = mine + lax.ppermute(theirs[0], "head", [(0, 1), (1, 0)]).astype(F32)
    back = [shift(summed[BACK - r].astype(BF16), "seq", -r) for r in range(1, BACK + 1)]
    total = summed[BACK]
    for piece in back:
        total = total + piece.astype(F32)
    if not halves:
        return grad_query, lax.psum_scatter(total.T, "head", scatter_dimension=0, tiled=True)
    return grad_query, total.T


def solution(mesh):
    placed = (
        P("seq", "head", None),
        P("seq", "head", None),
        P("seq", None),
        P("head", None, None),
        P("head", None, None),
        P("seq"),
    )
    return jax.shard_map(
        shards,
        mesh=mesh,
        in_specs=placed,
        out_specs=(P("seq", "head", None), P(("seq", "head"), None)),
        check_vma=False,
    )
```

time: 243 us -> 133 us (0.55)
  matrix products: 125 us -> 0 us
  Pallas kernels: 0 us -> 86.5 us
  other arithmetic: 51.5 us -> 4.62 us
  between operations: 14.3 us -> 0.71 us
  local copies, waits for them, and re-layouts: 17.4 us -> 3.91 us
  waiting for transfers between devices: 14.2 us -> 18.9 us
    dot_general x9 -> x0, matrix products: 125 us -> none  [the longest x1 22.5 us: shards(): jnp.einsum('thc,uc->htu', qcat, keys, preferred_element_type=jnp.float32)]
    pallas_call x0 -> x1, Pallas kernels: none -> 86.5 us  [shards(): pl.pallas_call(functools.partial(kernel, tokens, nope, latw, factor, halv...]
    sub x1 -> x2, other arithmetic: 33.2 us -> 1.23 us  [the longest x1 0.68 us: shards(): starts = doc_start - (lax.axis_index('seq') - BACK) * tokens]
    convert_element_type x1 -> x0, other arithmetic: 12.2 us -> none  [shards(): probs = (expo / jnp.sum(expo, -1, keepdims=True)).astype(jnp.bfloat16)]
    slice x9 -> x1, local copies, waits for them, and re-layouts: 5.5 us -> 0.09 us  [shards(): counts = ends - starts[::LANES] // LANES]
    ppermute x6 -> x7, waiting for transfers between devices: 14.2 us -> 18.9 us  [the longest x6 16.7 us: shift(): return lax.ppermute(block, axis, route)]
    reshape x8 -> x0, local copies, waits for them, and re-layouts: 4.38 us -> none  [the longest x6 3.05 us: shards(): piece.reshape(tokens, width)]
    concatenate x2 -> x1, other arithmetic: 3.69 us -> 1.17 us  [shards(): keys = jnp.concatenate(received + [own], 1)]
  transfers between devices with their start and end apart: 7 -> 7, of which waited for: 2 -> 7; matrix products, arithmetic and copies ran while one was open for 20% -> 4% of each run, Pallas kernels for 0% -> 0%
where the time goes in v1:
time: 133 us
  Pallas kernels  86.5 us (65%)
  waiting for transfers between devices  18.9 us (14%)
  starting transfers between devices  18.1 us (14%)
  other arithmetic  4.62 us (3%)
  local copies, waits for them, and re-layouts  3.91 us (3%)
    pallas_call x1, Pallas kernels, shards(): pl.pallas_call(functools.partial(kernel, tokens, nope, latw, factor, halv...  86.5 us
    ppermute x6, starting transfers between devices, shift(): return lax.ppermute(block, axis, route)  18 us
    ppermute x6, waiting for transfers between devices, shift(): return lax.ppermute(block, axis, route)  16.7 us
    unnamed x5, local copies, waits for them, and re-layouts  3.78 us
  transfers between devices with their start and end apart: 7, of which 7 were waited for; matrix products, arithmetic and copies ran while one was open for 4% of the time, Pallas kernels for 0%

profile of v1, /device:TPU:12, one launch (start us, length us, event | category | flops | bytes accessed | tf_op | source)
XLA Modules:
  0.0 132.8 jit_solution(15395565269527913078)
XLA Ops:
  0.6 3.4 %collective-permute-start.2 = (bf16[576,256]{1,0:T(8,128)(2,1)}, bf16[576,256]{1,0:T(8,128)(2,1)S(1)}, u32[]{:S(2)}, u32[]{:S(2)}) collective-permute-start(bf16[576,256]{1,0:T(8,128)(2,1)} %bitcast.28), channel_id=1, source_target_pairs={{0,2},{2,4},{4,6},{6,8},{8,10},{10,12},{12,14},{14,16},{16,18},{18... | collective-permute-start | bytes 884744 | tf_op jit(solution)/shard_map/ppermute | solution.py:107
  4.0 3.4 %collective-permute-start.1 = (bf16[576,256]{1,0:T(8,128)(2,1)}, bf16[576,256]{1,0:T(8,128)(2,1)S(1)}, u32[]{:S(2)}, u32[]{:S(2)}) collective-permute-start(bf16[576,256]{1,0:T(8,128)(2,1)} %bitcast.29), channel_id=1, source_target_pairs={{0,4},{2,6},{4,8},{6,10},{8,12},{10,14},{12,16},{14,18},{16,20},{1... | collective-permute-start | bytes 884744 | tf_op jit(solution)/shard_map/ppermute | solution.py:107
  7.5 4.4 %collective-permute-start = (bf16[576,256]{1,0:T(8,128)(2,1)}, bf16[576,256]{1,0:T(8,128)(2,1)S(1)}, u32[]{:S(2)}, u32[]{:S(2)}) collective-permute-start(bf16[576,256]{1,0:T(8,128)(2,1)} %bitcast.30), channel_id=1, source_target_pairs={{0,6},{2,8},{4,10},{6,12},{8,14},{10,16},{12,18},{14,20},{16,22},{... | collective-permute-start | bytes 884744 | tf_op jit(solution)/shard_map/ppermute | solution.py:107
  11.8 0.7 broadcast_subtract_fusion
  12.5 0.1 slice.18
  12.6 3.8 %copy.10 = bf16[256,32,128]{2,0,1:T(8,128)(2,1)} copy(bf16[256,32,128]{2,1,0:T(8,128)(2,1)} %param.7) | data formatting | bytes 4194304 | tf_op args[1]
  16.4 0.0 copy-done.1
  16.4 0.5 fusion.4.counts
  17.0 1.8 %collective-permute-done.2 = bf16[576,256]{1,0:T(8,128)(2,1)S(1)} collective-permute-done((bf16[576,256]{1,0:T(8,128)(2,1)}, bf16[576,256]{1,0:T(8,128)(2,1)S(1)}, u32[]{:S(2)}, u32[]{:S(2)}) %collective-permute-start.2) | collective-permute-done | bytes 294944 | tf_op jit(solution)/shard_map/ppermute | solution.py:107
  18.7 0.3 collective-permute-done.1
  19.0 6.9 %collective-permute-done = bf16[576,256]{1,0:T(8,128)(2,1)S(1)} collective-permute-done((bf16[576,256]{1,0:T(8,128)(2,1)}, bf16[576,256]{1,0:T(8,128)(2,1)S(1)}, u32[]{:S(2)}, u32[]{:S(2)}) %collective-permute-start) | collective-permute-done | bytes 294944 | tf_op jit(solution)/shard_map/ppermute | solution.py:107
  25.9 0.0 copy-done
  25.9 1.2 pad_maximum_fusion.kt_ref
  27.1 86.5 %attend.1 = (bf16[32,192,256]{2,1,0:T(8,128)(2,1)}, f32[4,576,128]{2,1,0:T(8,128)}, bf16[4,576,128]{2,1,0:T(8,128)(2,1)}) custom-call(s32[2]{0:T(128)} %fusion.4.counts, s32[1]{0:T(128)} %bitcast.side, s32[1,256]{1,0:T(1,128)} %bitcast.32, bf16[32,192,256]{2,1,0:T(8,128)(2,1)} %bitcast.27, bf16[32,256,128]{2,1,0:T(8,128)(2,1)} %bitcast.26, ...), custom_call_target="tpu_custom_call" | custom-call | tf_op jit(solution)/shard_map/attend/pallas_call | solution.py:135
  113.6 0.1 collective-permute-start.3
  113.6 2.2 %collective-permute-done.3 = bf16[4,576,128]{2,1,0:T(8,128)(2,1)S(1)} collective-permute-done((bf16[4,576,128]{2,1,0:T(8,128)(2,1)}, bf16[4,576,128]{2,1,0:T(8,128)(2,1)S(1)}, u32[]{:S(2)}, u32[]{:S(2)}) %collective-permute-start.3) | collective-permute-done | bytes 589856 | tf_op jit(solution)/shard_map/ppermute | solution.py:182
  115.8 1.4 %fusion.5 = (bf16[4,576,128]{2,1,0:T(8,128)(2,1)S(1)}, f32[4,576,128]{2,1,0:T(8,128)S(1)}) fusion(f32[4,576,128]{2,1,0:T(8,128)} %get-tuple-element.6, bf16[4,576,128]{2,1,0:T(8,128)(2,1)S(1)} %collective-permute-done.3), kind=kLoop, calls=%fused_computation.17 | loop fusion | flops 884736 | bytes 3538944 | tf_op jit(solution)/shard_map/convert.2
  117.3 1.9 %collective-permute-start.4 = (bf16[576,128]{1,0:T(8,128)(2,1)S(1)}, bf16[576,128]{1,0:T(8,128)(2,1)S(1)}, u32[]{:S(2)}, u32[]{:S(2)}) collective-permute-start(bf16[576,128]{1,0:T(8,128)(2,1)S(1)} %get-tuple-element.10), channel_id=1, source_target_pairs={{2,0},{4,2},{6,4},{8,6},{10,8},{12,10},{14,12},{16,14},{18,16},{20... | collective-permute-start | bytes 442376 | tf_op jit(solution)/shard_map/ppermute | solution.py:107
  119.3 1.9 %collective-permute-start.6 = (bf16[576,128]{1,0:T(8,128)(2,1)S(1)}, bf16[576,128]{1,0:T(8,128)(2,1)S(1)}, u32[]{:S(2)}, u32[]{:S(2)}) collective-permute-start(bf16[576,128]{1,0:T(8,128)(2,1)S(1)} %get-tuple-element.11), channel_id=1, source_target_pairs={{6,0},{8,2},{10,4},{12,6},{14,8},{16,10},{18,12},{20,14},{22,16},{... | collective-permute-start | bytes 442376 | tf_op jit(solution)/shard_map/ppermute | solution.py:107
  121.2 3.0 %collective-permute-start.5 = (bf16[576,128]{1,0:T(8,128)(2,1)S(1)}, bf16[576,128]{1,0:T(8,128)(2,1)S(1)}, u32[]{:S(2)}, u32[]{:S(2)}) collective-permute-start(bf16[576,128]{1,0:T(8,128)(2,1)S(1)} %get-tuple-element.12), channel_id=1, source_target_pairs={{4,0},{6,2},{8,4},{10,6},{12,8},{14,10},{16,12},{18,14},{20,16},{2... | collective-permute-start | bytes 442376 | tf_op jit(solution)/shard_map/ppermute | solution.py:107
  124.2 1.7 %collective-permute-done.4 = bf16[576,128]{1,0:T(8,128)(2,1)S(1)} collective-permute-done((bf16[576,128]{1,0:T(8,128)(2,1)S(1)}, bf16[576,128]{1,0:T(8,128)(2,1)S(1)}, u32[]{:S(2)}, u32[]{:S(2)}) %collective-permute-start.4) | collective-permute-done | bytes 147488 | tf_op jit(solution)/shard_map/ppermute | solution.py:107
  125.9 4.9 %collective-permute-done.6 = bf16[576,128]{1,0:T(8,128)(2,1)S(1)} collective-permute-done((bf16[576,128]{1,0:T(8,128)(2,1)S(1)}, bf16[576,128]{1,0:T(8,128)(2,1)S(1)}, u32[]{:S(2)}, u32[]{:S(2)}) %collective-permute-start.6) | collective-permute-done | bytes 147488 | tf_op jit(solution)/shard_map/ppermute | solution.py:107
  130.9 1.2 collective-permute-done.5
  132.0 0.8 fusion.3
  (3 shorter events, 0.0 us)
Async XLA Ops:
  0.6 18.1 %collective-permute-start.2 = (bf16[576,256]{1,0:T(8,128)(2,1)}, bf16[576,256]{1,0:T(8,128)(2,1)S(1)}, u32[]{:S(2)}, u32[]{:S(2)}) collective-permute-start(bf16[576,256]{1,0:T(8,128)(2,1)} %bitcast.28), channel_id=1, source_target_pairs={{0,2},{2,4},{4,6},{6,8},{8,10},{10,12},{12,14},{14,16},{16,18},{18... | collective-permute-start | bytes 884744 | tf_op jit(solution)/shard_map/ppermute | solution.py:107
  4.0 15.0 %collective-permute-start.1 = (bf16[576,256]{1,0:T(8,128)(2,1)}, bf16[576,256]{1,0:T(8,128)(2,1)S(1)}, u32[]{:S(2)}, u32[]{:S(2)}) collective-permute-start(bf16[576,256]{1,0:T(8,128)(2,1)} %bitcast.29), channel_id=1, source_target_pairs={{0,4},{2,6},{4,8},{6,10},{8,12},{10,14},{12,16},{14,18},{16,20},{1... | collective-permute-start | bytes 884744 | tf_op jit(solution)/shard_map/ppermute | solution.py:107
  7.5 18.4 %collective-permute-start = (bf16[576,256]{1,0:T(8,128)(2,1)}, bf16[576,256]{1,0:T(8,128)(2,1)S(1)}, u32[]{:S(2)}, u32[]{:S(2)}) collective-permute-start(bf16[576,256]{1,0:T(8,128)(2,1)} %bitcast.30), channel_id=1, source_target_pairs={{0,6},{2,8},{4,10},{6,12},{8,14},{10,16},{12,18},{14,20},{16,22},{... | collective-permute-start | bytes 884744 | tf_op jit(solution)/shard_map/ppermute | solution.py:107
  12.5 3.9 %copy-start.1 = (s32[256]{0:T(256)}, s32[256]{0:T(256)S(1)}, u32[]{:S(2)}) copy-start(s32[256]{0:T(256)S(1)} %broadcast_subtract_fusion) | copy-start | bytes 3076
  12.6 13.3 %copy-start = (bf16[256,576]{0,1:T(8,128)(2,1)S(1)}, bf16[256,576]{0,1:T(8,128)(2,1)}, u32[]{:S(2)}) copy-start(bf16[256,576]{0,1:T(8,128)(2,1)} %param.8) | copy-start | bytes 884740
  113.6 2.3 %collective-permute-start.3 = (bf16[4,576,128]{2,1,0:T(8,128)(2,1)}, bf16[4,576,128]{2,1,0:T(8,128)(2,1)S(1)}, u32[]{:S(2)}, u32[]{:S(2)}) collective-permute-start(bf16[4,576,128]{2,1,0:T(8,128)(2,1)} %get-tuple-element.7), channel_id=1, source_target_pairs={{0,1},{1,0},{2,3},{3,2},{4,5},{5,4},{6,7},{7,6},{8,9},{9,8},{10,11... | collective-permute-start | bytes 1769480 | tf_op jit(solution)/shard_map/ppermute | solution.py:182
  117.3 8.6 %collective-permute-start.4 = (bf16[576,128]{1,0:T(8,128)(2,1)S(1)}, bf16[576,128]{1,0:T(8,128)(2,1)S(1)}, u32[]{:S(2)}, u32[]{:S(2)}) collective-permute-start(bf16[576,128]{1,0:T(8,128)(2,1)S(1)} %get-tuple-element.10), channel_id=1, source_target_pairs={{2,0},{4,2},{6,4},{8,6},{10,8},{12,10},{14,12},{16,14},{18,16},{20... | collective-permute-start | bytes 442376 | tf_op jit(solution)/shard_map/ppermute | solution.py:107
  119.3 11.6 %collective-permute-start.6 = (bf16[576,128]{1,0:T(8,128)(2,1)S(1)}, bf16[576,128]{1,0:T(8,128)(2,1)S(1)}, u32[]{:S(2)}, u32[]{:S(2)}) collective-permute-start(bf16[576,128]{1,0:T(8,128)(2,1)S(1)} %get-tuple-element.11), channel_id=1, source_target_pairs={{6,0},{8,2},{10,4},{12,6},{14,8},{16,10},{18,12},{20,14},{22,16},{... | collective-permute-start | bytes 442376 | tf_op jit(solution)/shard_map/ppermute | solution.py:107
  121.2 10.8 %collective-permute-start.5 = (bf16[576,128]{1,0:T(8,128)(2,1)S(1)}, bf16[576,128]{1,0:T(8,128)(2,1)S(1)}, u32[]{:S(2)}, u32[]{:S(2)}) collective-permute-start(bf16[576,128]{1,0:T(8,128)(2,1)S(1)} %get-tuple-element.12), channel_id=1, source_target_pairs={{4,0},{6,2},{8,4},{10,6},{12,8},{14,10},{16,12},{18,14},{20,16},{2... | collective-permute-start | bytes 442376 | tf_op jit(solution)/shard_map/ppermute | solution.py:107
